TPU v7x, 256 devices: a whole 4x4x8 slice. The times are simulated.
256 devices in a mesh: group: 8 (over z), mp: 32 (over y, x, core).
Axes of the slice: x: 4, y: 4, z: 8, core: 2. Of those that a mesh axis runs over, the one named last changes fastest.
Arguments:
- option_latent_states: bfloat16 [2048, 8192], P('group', 'mp'), may hold values from -6 to 6
- mixer_scaling_factor: bfloat16 [1, 8192], P(None, 'mp'), may hold values from 0.099609375 to 1.8984375
- question_mapping_matrix: bfloat16 [8192, 8192], P(None, 'mp'), may hold values from -0.0625 to 0.0625
- lookup_content_matrix: bfloat16 [8192, 2048], P(None, 'mp'), may hold values from -0.0625 to 0.0625
- final_mapping_matrix: bfloat16 [8192, 8192], P('mp'), may hold values from -0.125 to 0.125
- payoff_readout_vector: bfloat16 [8192], P('mp'), may hold values from -0.0625 to 0.0625
- shared_trie_memo: bfloat16 [2, 512, 128, 1024], P(None, ('group', 'mp')), may hold values from -100 to 100
- option_route_pages: int32 [128, 32], P('group'), may hold values from 0 to 63, as said below
- option_page_tally: int32 [128], P('group'), may hold values from 1 to 32, as said below
- option_token_span: int32 [128], P('group'), may hold values from 1 to 16
- retained_pages: int32 [512], P(('group', 'mp')), may hold values from 0 to 1
- growth_place_mapping: int32 [768], P(('group', 'mp')), may hold values from 0 to 15, as said below
Outputs:
- scored_rows: bfloat16 [2048, 8192], P('group', 'mp')
- rewards: float32 [128], P('group')
- expanded: bfloat16 [2, 768, 128, 1024], P(None, ('group', 'mp'))
Inputs may be any that keep to these rules, and one draw needn't show every extreme that they name: `option_route_pages`: the t-th listed block of a candidate is one of t * 2 to (t + 1) * 2 - 1; entries at or past option_page_tally are not read. `option_page_tally`: among the 16 candidates of each group index one lists all 32 blocks. `growth_place_mapping`: for every mp index, every survivor of every group index fills some slot.
All inputs are finite; a program needn't handle non-finite values.
Results may differ from a plain program's by a relative error of at most 0.005.
The roundings to bfloat16 on the way count: a program that leaves them out, or rounds other values in their place, can miss the bound.
Values may be sent and summed in bfloat16 or wider, within the bound.
No kernel may reach another device: no remote copies, remote signals or barrier semaphores. Data moves between devices by JAX's collectives and lax.ppermute only.
A program may use at most 128 MiB of HBM per device.

v0:
```python
import jax
import jax.numpy as jnp
from jax import lax
from jax.sharding import Mesh
from jax.sharding import PartitionSpec as P

D = 8192
HEADS = 64
KVH = 8
HD = 128
BLK = 128
STEP = 16
MP = ("mp_0", "mp_1", "mp_2")
GROUP_MP = ("group", "mp_0", "mp_1", "mp_2")
epsilon = 1e-06
masked_value = -1e30


def sent_together(arrays, axis, dim, along):
    ends, at = ([], 0)
    for a in arrays[:-1]:
        at += a.shape[along]
        ends.append(at)
    both = jnp.concatenate(arrays, axis=along)
    return tuple(jnp.split(lax.all_gather(both, axis, axis=dim, tiled=True), ends, axis=along))


def in_order(tiles, dim):
    lengths = list(tiles.shape[1:])
    lengths[dim] *= tiles.shape[0]
    return jnp.moveaxis(tiles, 0, dim).reshape(lengths)


def from_everyone(x, axis):
    copies = jnp.broadcast_to(x, (lax.axis_size(axis), *x.shape))
    return lax.all_to_all(copies, axis, split_axis=0, concat_axis=0, tiled=True)


def collect(x, axis, dim):
    return in_order(from_everyone(x, axis), dim)


def split_up(x, dim, count):
    before, after = (x.shape[:dim], x.shape[dim + 1 :])
    return jnp.moveaxis(x.reshape(*before, count, -1, *after), dim, 0)


def scatter_pairs(x, chips, core, dim):
    sizes = (lax.axis_size(chips), lax.axis_size(core))
    tiles = split_up(x, dim, sizes[0] * sizes[1])
    inside = tiles.shape[1:]
    tiles = tiles.reshape(*sizes, *inside).swapaxes(0, 1).reshape(-1, *inside)
    tiles = lax.psum_scatter(tiles, core, scatter_dimension=0, tiled=True)
    return lax.psum_scatter(tiles, chips, scatter_dimension=0, tiled=True)[0]


def over_copies(x, axis):
    everything = from_everyone(x, axis)
    return jnp.sum(everything, axis=0)


def local(
    option_latent_states,
    mixer_scaling_factor,
    question_mapping_matrix,
    lookup_content_matrix,
    final_mapping_matrix,
    payoff_readout_vector,
    shared_trie_memo,
    option_route_pages,
    option_page_tally,
    option_token_span,
    retained_pages,
    growth_place_mapping,
):
    width_mp = lax.axis_size(MP)
    my_index = lax.axis_index(MP)
    received = lax.all_to_all(
        option_latent_states, "group", split_axis=0, concat_axis=0, tiled=True
    )
    row_total = received.shape[0]
    cand_here = row_total // STEP
    heads_here = question_mapping_matrix.shape[1] // HD
    group_size = HEADS // KVH
    pair_head = my_index * heads_here // group_size
    score_scale = HD ** (-0.5)
    row_piece, gain_piece = sent_together((received, mixer_scaling_factor), MP, 1, 0)
    piece_wide = row_piece.astype(jnp.float32)
    scaled = (piece_wide * gain_piece.astype(jnp.float32)).astype(jnp.bfloat16)
    query_sum = jnp.dot(scaled, question_mapping_matrix, preferred_element_type=jnp.float32)
    pair_sum = lax.dot_general(
        lookup_content_matrix, scaled, (((0,), (1,)), ((), ())), preferred_element_type=jnp.float32
    )
    square_sum = jnp.sum(piece_wide * piece_wide, axis=1)
    query_sum, pair_sum, square_sum = (query_sum, pair_sum, square_sum)
    inv_rms = lax.rsqrt(square_sum / D + epsilon)
    queries = (query_sum * inv_rms[:, None]).astype(jnp.bfloat16)
    pair_part = (pair_sum * inv_rms[None, :]).astype(jnp.bfloat16)
    fresh_pairs = collect(pair_part, MP, 0)
    fresh_keys = lax.dynamic_slice_in_dim(fresh_pairs, pair_head * HD, HD, 0).reshape(
        HD, cand_here, STEP
    )
    fresh_values = lax.dynamic_slice_in_dim(fresh_pairs, (KVH + pair_head) * HD, HD, 0).reshape(
        HD, cand_here, STEP
    )
    own_queries = queries.reshape(cand_here, STEP, heads_here, HD)
    position = jnp.arange(STEP, dtype=jnp.int32)
    own_mask = (position[None, None, :] <= position[None, :, None]) & (
        position[None, None, :] < option_token_span[:, None, None]
    )
    own_score = (
        jnp.einsum("csjd,dcu->jcsu", own_queries, fresh_keys, preferred_element_type=jnp.float32)
        * score_scale
    )
    own_score = jnp.where(own_mask[None], own_score, masked_value)
    own_top = jnp.max(own_score, axis=-1).reshape(heads_here, row_total)
    pool_here = shared_trie_memo.shape[1]
    pool_group = pool_here * width_mp
    listed = (
        jnp.arange(option_route_pages.shape[1], dtype=jnp.int32)[None, :]
        < option_page_tally[:, None]
    )
    member = jnp.any(
        (option_route_pages[:, :, None] == jnp.arange(pool_group, dtype=jnp.int32)[None, None, :])
        & listed[:, :, None],
        axis=1,
    )
    spread = shared_trie_memo.reshape(2, pool_here, BLK, KVH, 1, HD)
    spread = jnp.broadcast_to(spread, (2, pool_here, BLK, KVH, width_mp // KVH, HD)).reshape(
        2, pool_here, BLK, width_mp, HD
    )
    head_pool = lax.all_to_all(spread, MP, split_axis=3, concat_axis=1, tiled=True)
    path_keys = head_pool[0].reshape(pool_group * BLK, HD)
    path_values = head_pool[1].reshape(pool_group * BLK, HD)
    path_mask = jnp.broadcast_to(
        member[:, None, :, None], (cand_here, STEP, pool_group, BLK)
    ).reshape(row_total, pool_group * BLK)
    my_queries = queries.reshape(row_total, heads_here, HD)
    sum_list = []
    total_list = []
    top_list = []
    for head_index in range(heads_here):
        head_score = (
            jnp.einsum(
                "rd,pd->rp",
                my_queries[:, head_index],
                path_keys,
                preferred_element_type=jnp.float32,
            )
            * score_scale
        )
        head_score = jnp.where(path_mask, head_score, masked_value)
        head_top = jnp.maximum(jnp.max(head_score, axis=-1), own_top[head_index])
        head_mass = jnp.where(path_mask, jnp.exp(head_score - head_top[:, None]), 0.0)
        sum_list.append(
            jnp.dot(head_mass.astype(jnp.bfloat16), path_values, preferred_element_type=jnp.float32)
        )
        total_list.append(jnp.sum(head_mass, axis=-1))
        top_list.append(head_top)
    path_sum = jnp.stack(sum_list)
    path_total = jnp.stack(total_list)
    row_top = jnp.stack(top_list)
    top_grid = row_top.reshape(heads_here, cand_here, STEP)[..., None]
    own_mass = jnp.where(own_mask[None], jnp.exp(own_score - top_grid), 0.0)
    own_sum = jnp.einsum(
        "jcsu,dcu->jcsd",
        own_mass.astype(jnp.bfloat16),
        fresh_values,
        preferred_element_type=jnp.float32,
    ).reshape(heads_here, row_total, HD)
    own_total = jnp.sum(own_mass, axis=-1).reshape(heads_here, row_total)
    attended = ((path_sum + own_sum) / (path_total + own_total)[..., None]).astype(jnp.bfloat16)
    partial_value = jnp.einsum(
        "jrd,jdf->rf",
        attended,
        final_mapping_matrix.reshape(heads_here, HD, D),
        preferred_element_type=jnp.float32,
    )
    projected = scatter_pairs(partial_value, ("mp_0", "mp_1"), "mp_2", 1)
    live_rows = (position[None, :] < option_token_span[:, None]).reshape(row_total)
    scored_rows = (projected * live_rows[:, None].astype(jnp.float32)).astype(jnp.bfloat16)
    last_row = (position[None, :] == option_token_span[:, None] - 1).astype(jnp.float32)
    last_values = jnp.sum(projected.reshape(cand_here, STEP, -1) * last_row[:, :, None], axis=1)
    partial_reward = jnp.sum(
        last_values * payoff_readout_vector.astype(jnp.float32)[None, :], axis=1
    )
    rewards = over_copies(partial_reward, MP)
    gathered_elements = jnp.take(shared_trie_memo, retained_pages, axis=1)
    gathered = lax.all_gather(gathered_elements, "group", axis=1, tiled=True)
    expanded = jnp.take(gathered, growth_place_mapping, axis=1)
    return (scored_rows, rewards, expanded)


def solution(mesh):
    split = Mesh(
        mesh.devices.reshape(mesh.shape["group"], 4, 4, 2), ("group", "mp_0", "mp_1", "mp_2")
    )
    in_specs = (
        P("group", MP),
        P(None, MP),
        P(None, MP),
        P(None, MP),
        P(MP, None),
        P(MP),
        P(None, GROUP_MP, None, None),
        P("group", None),
        P("group"),
        P("group"),
        P(GROUP_MP),
        P(GROUP_MP),
    )
    out_specs = (P("group", MP), P("group"), P(None, GROUP_MP, None, None))
    return jax.shard_map(local, mesh=split, in_specs=in_specs, out_specs=out_specs, check_vma=False)
```

profile of v0, /device:TPU:1, one launch (start us, length us, event | category | flops | bytes accessed | tf_op | source)
XLA Modules:
  0.0 321.8 jit_solution(12386661473913503255)
XLA Ops:
  8.1 16.9 %all_to_all.38 = bf16[8,32,256]{2,1,0:T(8,128)(2,1)S(1)} all-to-all(bf16[8,32,256]{2,1,0:T(8,128)(2,1)} %bitcast.140), channel_id=1, replica_groups=mesh['group'=8,'mp_0'=4,'mp_1'=4,'mp_2'=2] {'group'}, dimensions={0} | all-to-all | bytes 262144 | tf_op jit(solution)/shard_map/all_to_all | solution.py:78
  25.0 1.3 pad_maximum_fusion
  26.3 0.3 copy_bitcast_fusion.1
  26.6 3.2 %broadcast_in_dim.94 = bf16[2,2,128,8,4,128]{5,2,1,0,4,3:T(8,128)(2,1)} broadcast(bf16[2,2,128,8,128]{4,2,1,0,3:T(8,128)(2,1)S(1)} %copy_bitcast_fusion.1), dimensions={0,1,2,3,5} | broadcast | bytes 5242880 | tf_op jit(solution)/shard_map/broadcast_in_dim | solution.py:129
  29.8 9.4 %all-to-all-start.1 = ((bf16[2,2,128,32,128]{4,2,1,0,3:T(8,128)(2,1)}), bf16[2,2,128,32,128]{4,2,1,0,3:T(8,128)(2,1)}, u32[]{:S(2)}, u32[]{:S(2)}) async-start(bf16[2,2,128,32,128]{4,2,1,0,3:T(8,128)(2,1)} %bitcast.123), calls=%async_computation.1 | async-start | bytes 8388608 | tf_op jit(solution)/shard_map/all_to_all | solution.py:132
  39.4 6.4 %copy.103 = bf16[8192,128,2]{1,0,2:T(8,128)(2,1)} copy(bf16[8192,128,2]{0,1,2:T(8,128)(2,1)} %bitcast.132) | data formatting | bytes 8388608 | tf_op jit(solution)/shard_map/jrd,jdf->rf/dot_general | solution.py:173
  46.2 45.6 %all-to-all-done.1 = bf16[2,2,128,32,128]{4,2,1,0,3:T(8,128)(2,1)} async-done(((bf16[2,2,128,32,128]{4,2,1,0,3:T(8,128)(2,1)}), bf16[2,2,128,32,128]{4,2,1,0,3:T(8,128)(2,1)}, u32[]{:S(2)}, u32[]{:S(2)}) %all-to-all-start.1) | async-done | bytes 4194336 | tf_op jit(solution)/shard_map/all_to_all | solution.py:132
  91.8 2.5 copy.135
  94.3 2.3 fusion.64
  96.6 18.1 %all-gather.3.cloned.1.call-done = bf16[257,8192]{1,0:T(8,128)(2,1)} async-done(((bf16[257,256]{1,0:T(8,128)(2,1)}), bf16[257,8192]{1,0:T(8,128)(2,1)}) %all-gather.3.cloned.1.call-update) | async-done | bytes 4210704 | tf_op jit(solution)/shard_map/all_gather | solution.py:25
  114.7 3.1 fusion.3
  117.8 0.9 slice_convert_fusion
  118.7 3.6 %fusion.40 = bf16[64,256]{1,0:T(8,128)(2,1)S(1)} fusion(bf16[8192,64]{0,1:T(8,128)(2,1)S(1)} %copy-done.10, f32[8192]{0:T(1024)S(1)} %bitcast.147, bf16[257,8192]{1,0:T(8,128)(2,1)} %all-gather.3.cloned.1.call-done, f32[256]{0:T(256)S(1)} %add_rsqrt_fusion), kind=kOutput, calls=%fused_computation.36 | convolution fusion | flops 274759680 | bytes 5309440 | tf_op jit(solution)/shard_map/dot_general | solution.py:91
  122.3 1.1 broadcast_in_dim.97
  123.4 5.5 %all-to-all-start.2 = ((bf16[32,64,256]{2,1,0:T(8,128)(2,1)}), bf16[32,64,256]{2,1,0:T(8,128)(2,1)}, u32[]{:S(2)}, u32[]{:S(2)}) async-start(bf16[32,64,256]{2,1,0:T(8,128)(2,1)} %broadcast_in_dim.97), calls=%async_computation.2 | async-start | bytes 2097152 | tf_op jit(solution)/shard_map/all_to_all | solution.py:36
  129.1 5.4 %fusion.25 = bf16[256,256]{0,1:T(8,128)(2,1)S(1)} fusion(bf16[8192,256]{1,0:T(8,128)(2,1)} %param.14, f32[8192]{0:T(1024)S(1)} %bitcast.148, bf16[257,8192]{1,0:T(8,128)(2,1)} %all-gather.3.cloned.1.call-done, f32[256]{0:T(256)S(1)} %add_rsqrt_fusion), kind=kOutput, calls=%fused_computation.31 | convolution fusion | flops 1080164352 | bytes 8553472 | tf_op jit(solution)/shard_map/dot_general | solution.py:90
  134.6 0.7 reshape.267
  135.3 0.6 broadcast_in_dim.92
  135.9 7.5 %fusion.68 = (f32[256]{0:T(256)S(1)}, f32[256,8192]{1,0:T(8,128)}) fusion(bf16[8192,128]{1,0:T(8,128)(2,1)} %bitcast.135, bf16[256,2,128]{0,2,1:T(8,128)(2,1)S(1)} %bitcast.141, pred[32,8,64,128]{3,2,1,0:T(32,128)(4,1)S(1)} %bitcast.127), kind=kOutput, calls=%fused_computation.91 | convolution fusion | flops 543162112 | bytes 12649472 | tf_op jit(solution)/shard_map/rd,pd->rp/dot_general | solution.py:144
  143.5 7.5 %fusion.66 = (f32[256]{0:T(256)S(1)}, f32[256,8192]{1,0:T(8,128)}) fusion(bf16[8192,128]{1,0:T(8,128)(2,1)} %bitcast.136, bf16[256,2,128]{0,2,1:T(8,128)(2,1)S(1)} %bitcast.142, pred[32,8,64,128]{3,2,1,0:T(32,128)(4,1)S(1)} %bitcast.128), kind=kOutput, calls=%fused_computation.89 | convolution fusion | flops 543162112 | bytes 12649472 | tf_op jit(solution)/shard_map/rd,pd->rp/dot_general | solution.py:144
  151.1 0.9 constant_dynamic-slice_fusion
  152.0 0.7 copy.94
  152.7 1.4 fusion.67
  154.1 0.6 squeeze.20
  154.8 1.3 max.34
  156.0 0.6 squeeze.22
  156.7 0.7 max.35
  157.4 7.5 %fusion.28 = f32[1,256,128]{2,1,0:T(8,128)} fusion(bf16[8192,128]{1,0:T(8,128)(2,1)} %bitcast.133, f32[256,8192]{1,0:T(8,128)} %get-tuple-element.37, f32[256]{0:T(256)} %max.34, pred[32,8,64,128]{3,2,1,0:T(32,128)(4,1)S(1)} %bitcast.129), kind=kOutput, calls=%fused_computation.32 | convolution fusion | flops 543162368 | bytes 12715008 | tf_op jit(solution)/shard_map/dot_general | solution.py:156
  164.9 7.6 %fusion.4 = (f32[256]{0:T(256)}, f32[256]{0:T(256)}) fusion(f32[256,8192]{1,0:T(8,128)S(1)} %copy-done.1, f32[256]{0:T(256)S(1)} %copy-done.4, pred[32,8,64,128]{3,2,1,0:T(32,128)(4,1)S(1)} %bitcast.130, f32[256,8192]{1,0:T(8,128)} %get-tuple-element.33, f32[256]{0:T(256)S(1)} %max.35), kind=kLoop, calls=%fused_computation.12 | loop fusion | flops 12582400 | bytes 18878464 | tf_op jit(solution)/shard_map/reduce_sum | solution.py:158
  172.5 3.7 %fusion.31 = f32[1,256,128]{2,1,0:T(8,128)} fusion(bf16[8192,128]{1,0:T(8,128)(2,1)S(1)} %bitcast.134, f32[256,8192]{1,0:T(8,128)S(1)} %bitcast.126, f32[256]{0:T(256)S(1)} %max.35, pred[32,8,64,128]{3,2,1,0:T(32,128)(4,1)S(1)} %bitcast.131), kind=kOutput, calls=%fused_computation.33 | convolution fusion | flops 543162368 | bytes 12715008 | tf_op jit(solution)/shard_map/dot_general | solution.py:156
  176.9 0.7 maximum_add_fusion.1
  177.5 1.1 fusion.44
  178.7 3.5 %fusion.51 = f32[256,32,256,1]{2,0,1,3:T(8,128)S(1)} fusion(bf16[32,256,128,2]{2,1,0,3:T(8,128)(2,1)} %bitcast.120, bf16[2,256,128]{2,1,0:T(8,128)(2,1)S(1)} %fusion.44), kind=kOutput, calls=%fused_computation.52 | convolution fusion | flops 1073741824 | bytes 12713984 | tf_op jit(solution)/shard_map/jrd,jdf->rf/dot_general | solution.py:173
  182.1 3.8 %copy.105 = f32[2,16,256,256]{3,2,1,0:T(8,128)} copy(f32[2,16,256,256]{3,2,0,1:T(8,128)S(1)} %bitcast.121) | data formatting | bytes 16777216 | tf_op jit(solution)/shard_map/transpose | solution.py:52
  186.0 0.6 copy-done.11
  186.6 0.6 gather_fusion
  187.3 1.1 select_bitcast_fusion.1
  188.5 21.2 %reduce-scatter.5.cloned.1.call-done = f32[16,256,256]{2,1,0:T(8,128)} async-done(((f32[32,256,256]{2,1,0:T(8,128)}), f32[16,256,256]{2,1,0:T(8,128)}) %reduce-scatter.5.cloned.1.call-update) | async-done | bytes 4194320 | tf_op jit(solution)/shard_map/reduce_scatter | solution.py:53
  209.9 73.9 %all-gather.5.cloned.1.call-done = bf16[2,16,128,1024]{3,2,0,1:T(8,128)(2,1)} async-done(((bf16[2,2,128,1024]{3,2,0,1:T(8,128)(2,1)}), bf16[2,16,128,1024]{3,2,0,1:T(8,128)(2,1)}) %all-gather.5.cloned.1.call-update) | async-done | bytes 8388624 | tf_op jit(solution)/shard_map/all_gather | solution.py:189
  283.8 8.2 %copy.107 = bf16[2,16,128,1024]{3,2,1,0:T(8,128)(2,1)} copy(bf16[2,16,128,1024]{3,2,0,1:T(8,128)(2,1)} %all-gather.5.cloned.1.call-done) | data formatting | bytes 16777216 | tf_op jit(solution)/shard_map/all_gather | solution.py:189
  292.0 4.1 %gather_fusion.1 = bf16[3,2,128,1024]{3,2,1,0:T(8,128)(2,1)S(1)} fusion(bf16[2,16,128,1024]{3,2,1,0:T(8,128)(2,1)} %copy.107, s32[1024]{0:T(1024)S(1)} %pad_clamp_fusion), kind=kCustom, calls=%fused_computation.1 | custom fusion | bytes 3145740 | tf_op jit(solution)/shard_map/jit(_take)/gather | solution.py:190
  296.4 1.3 copy.108
  297.6 1.1 multiply_reduce_fusion
  298.8 0.6 broadcast_in_dim.101
  299.5 7.7 %all-to-all-start.3 = ((f32[32,1,16]{2,1,0:T(1,128)}), f32[32,1,16]{2,1,0:T(1,128)S(1)}, u32[]{:S(2)}, u32[]{:S(2)}) async-start(f32[32,1,16]{2,1,0:T(1,128)} %broadcast_in_dim.101), calls=%async_computation.4 | async-start | bytes 32768 | tf_op jit(solution)/shard_map/all_to_all | solution.py:36
  307.2 1.7 fusion.45
  308.9 5.3 %all-to-all-done.3 = f32[32,1,16]{2,1,0:T(1,128)S(1)} async-done(((f32[32,1,16]{2,1,0:T(1,128)}), f32[32,1,16]{2,1,0:T(1,128)S(1)}, u32[]{:S(2)}, u32[]{:S(2)}) %all-to-all-start.3) | async-done | bytes 2080 | tf_op jit(solution)/shard_map/all_to_all | solution.py:36
  314.1 0.6 reduce_sum.69
  (74 shorter events, 2.4 us)
Async XLA Ops:
  8.0 18.3 %copy-start = (bf16[2,2,128,1024]{3,2,1,0:T(8,128)(2,1)S(1)}, bf16[2,2,128,1024]{3,2,1,0:T(8,128)(2,1)}, u32[]{:S(2)}) copy-start(bf16[2,2,128,1024]{3,2,1,0:T(8,128)(2,1)} %param.18) | copy-start | bytes 3145732
  8.0 106.6 %all-gather.3.cloned.1.call-start = ((), (), s32[]{:S(2)}) async-start(), calls=%async_computation.6 | async-start | bytes 4460544 | tf_op jit(solution)/shard_map/all_gather | solution.py:25
  29.8 61.9 %all-to-all-start.1 = ((bf16[2,2,128,32,128]{4,2,1,0,3:T(8,128)(2,1)}), bf16[2,2,128,32,128]{4,2,1,0,3:T(8,128)(2,1)}, u32[]{:S(2)}, u32[]{:S(2)}) async-start(bf16[2,2,128,32,128]{4,2,1,0,3:T(8,128)(2,1)} %bitcast.123), calls=%async_computation.1 | async-start | bytes 8388608 | tf_op jit(solution)/shard_map/all_to_all | solution.py:132
  39.3 6.4 %copy-start.7 = (s32[16]{0:T(128)S(1)}, s32[16]{0:T(128)}, u32[]{:S(2)}) copy-start(s32[16]{0:T(128)} %param.20) | copy-start | bytes 196
  39.3 6.5 %copy-start.3 = (s32[16,32]{1,0:T(8,128)S(1)}, s32[16,32]{1,0:T(8,128)}, u32[]{:S(2)}) copy-start(s32[16,32]{1,0:T(8,128)} %param.19) | copy-start | bytes 6148
  39.3 6.7 %copy-start.8 = (s32[16]{0:T(128)S(1)}, s32[16]{0:T(128)}, u32[]{:S(2)}) copy-start(s32[16]{0:T(128)} %param.21) | copy-start | bytes 196
  96.6 22.1 %copy-start.10 = (bf16[8192,64]{0,1:T(8,128)(2,1)S(1)}, bf16[8192,64]{0,1:T(8,128)(2,1)}, u32[]{:S(2)}) copy-start(bf16[8192,64]{0,1:T(8,128)(2,1)} %param.15) | copy-start | bytes 3145732
  123.4 27.7 %all-to-all-start.2 = ((bf16[32,64,256]{2,1,0:T(8,128)(2,1)}), bf16[32,64,256]{2,1,0:T(8,128)(2,1)}, u32[]{:S(2)}, u32[]{:S(2)}) async-start(bf16[32,64,256]{2,1,0:T(8,128)(2,1)} %broadcast_in_dim.97), calls=%async_computation.2 | async-start | bytes 2097152 | tf_op jit(solution)/shard_map/all_to_all | solution.py:36
  128.9 80.7 %reduce-scatter.5.cloned.1.call-start = ((), (), s32[]{:S(2)}) async-start(), calls=%async_computation.7 | async-start | bytes 12582912 | tf_op jit(solution)/shard_map/reduce_scatter | solution.py:53
  143.4 7.6 %copy-start.6 = (f32[256]{0:T(256)}, f32[256]{0:T(256)S(1)}, u32[]{:S(2)}) copy-start(f32[256]{0:T(256)S(1)} %get-tuple-element.36) | copy-start | bytes 3076
  151.0 3.1 copy-start.5
  157.4 7.5 %copy-start.1 = (f32[256,8192]{1,0:T(8,128)S(1)}, f32[256,8192]{1,0:T(8,128)}, u32[]{:S(2)}) copy-start(f32[256,8192]{1,0:T(8,128)} %get-tuple-element.37) | copy-start | bytes 25165828
  157.4 7.5 %copy-start.4 = (f32[256]{0:T(256)S(1)}, f32[256]{0:T(256)}, u32[]{:S(2)}) copy-start(f32[256]{0:T(256)} %max.34) | copy-start | bytes 3076
  157.4 15.1 %slice-start = ((s8[8388608]{0:T(1024)(128)(4,1)}), s8[4194304]{0:T(1024)(128)(4,1)S(1)}, s32[]{:S(2)}) async-start(s8[8388608]{0:T(1024)(128)(4,1)} %bitcast.125), calls=%async_computation.10 | async-start | bytes 8388608
  164.9 7.6 %slice-start.1 = ((s8[8388608]{0:T(1024)(128)(4,1)}), s8[4194304]{0:T(1024)(128)(4,1)S(1)}, s32[]{:S(2)}) async-start(s8[8388608]{0:T(1024)(128)(4,1)} %bitcast.125), calls=%async_computation.11 | async-start | bytes 8388608
  164.9 7.6 %copy-start.2 = (bf16[1,32,2,128,1,128]{5,3,2,1,4,0:T(8,128)(2,1)S(1)}, bf16[1,32,2,128,1,128]{5,3,2,1,4,0:T(8,128)(2,1)}, u32[]{:S(2)}) copy-start(bf16[1,32,2,128,1,128]{5,3,2,1,4,0:T(8,128)(2,1)} %get-tuple-element.24) | copy-start | bytes 6291460
  185.9 0.7 copy-start.11
  185.9 97.8 %all-gather.5.cloned.1.call-start = ((), (), s32[]{:S(2)}) async-start(), calls=%async_computation.8 | async-start | bytes 9437184 | tf_op jit(solution)/shard_map/all_gather | solution.py:189
  187.2 22.5 %copy-start.12 = (bf16[256]{0:T(256)(128)(2,1)S(1)}, bf16[256]{0:T(256)(128)(2,1)}, u32[]{:S(2)}) copy-start(bf16[256]{0:T(256)(128)(2,1)} %param.17) | copy-start | bytes 1540
  187.2 22.5 %copy-start.13 = (s32[3]{0:T(128)S(1)}, s32[3]{0:T(128)}, u32[]{:S(2)}) copy-start(s32[3]{0:T(128)} %param.23) | copy-start | bytes 40
  187.2 22.6 %copy-start.9 = (s32[16]{0:T(128)S(1)}, s32[16]{0:T(128)}, u32[]{:S(2)}) copy-start(s32[16]{0:T(128)} %param.21) | copy-start | bytes 196
  188.4 109.2 %reduce-scatter.7.cloned.1.call-start = ((), (), s32[]{:S(2)}) async-start(), calls=%async_computation.9 | async-start | bytes 4456448
  299.5 14.7 %all-to-all-start.3 = ((f32[32,1,16]{2,1,0:T(1,128)}), f32[32,1,16]{2,1,0:T(1,128)S(1)}, u32[]{:S(2)}, u32[]{:S(2)}) async-start(f32[32,1,16]{2,1,0:T(1,128)} %broadcast_in_dim.101), calls=%async_computation.4 | async-start | bytes 32768 | tf_op jit(solution)/shard_map/all_to_all | solution.py:36
Sparse Core Ops, SparseCore 0:
  26.4 88.1 all-gather.2
  186.1 23.5 reduce-scatter.4
  213.3 82.5 reduce-scatter.6
Sparse Core Ops, SparseCore 1:
  188.8 94.9 all-gather.4
where the time goes:
time: 323 us; the launch traced here: 322 us
  waiting for transfers between devices  164 us (51%)
  matrix products  40.3 us (12%)
  local copies, waits for them, and re-layouts  39.9 us (12%)
  starting transfers between devices  23 us (7%)
  other arithmetic  22.2 us (7%)
  blocking collectives  16.9 us (5%)
  between operations  15.5 us (5%)
    all_gather x1, waiting for transfers between devices, local(): gathered = lax.all_gather(gathered_elements, 'group', axis=1, tiled=True)  73.9 us
    all_to_all x1, waiting for transfers between devices, local(): lax.all_to_all(spread, MP, split_axis=3, concat_axis=1, tiled=True)  45.6 us
    reduce_scatter x1, waiting for transfers between devices, scatter_pairs(): tiles = lax.psum_scatter(tiles, core, scatter_dimension=0, tiled=True)  21.2 us
    all_gather x1, waiting for transfers between devices, sent_together(): lax.all_gather(both, axis, axis=dim, tiled=True)  18.1 us
    all_to_all x1, blocking collectives, local(): lax.all_to_all(option_latent_states, 'group', split_axis=0, concat_axis=0...  16.9 us
    dot_general x2, matrix products, local(): jnp.einsum('rd,pd->rp', my_queries[:, head_index], path_keys, preferred_e...  15 us
    all_to_all x2, starting transfers between devices, from_everyone(): return lax.all_to_all(copies, axis, split_axis=0, concat_axis=0, tiled=True)  13.2 us
    dot_general x2, matrix products, local(): jnp.dot(head_mass.astype(jnp.bfloat16), path_values, preferred_element_ty...  11.2 us
  transfers between devices with their start and end apart: 7, of which 5 were waited for; matrix products, arithmetic and copies ran while one was open for 17% of the time, Pallas kernels for 0%

commit v1 on v0

--- a/solution.py
+++ b/solution.py
@@ -14,6 +14,40 @@
 GROUP_MP = ("group", "mp_0", "mp_1", "mp_2")
 epsilon = 1e-06
 masked_value = -1e30
+
+
+def derive_object(block_in, dim_i):
+    block_in = jnp.moveaxis(block_in, 0, dim_i)
+    all_values = block_in.shape
+    return block_in.reshape(
+        *all_values[:dim_i], all_values[dim_i] * all_values[dim_i + 1], *all_values[dim_i + 2 :]
+    )
+
+
+def sheet_write(vec, mesh_ax, axis_k):
+    slots = lax.psum(1, mesh_ax)
+    gallery = []
+    dd = 0
+    while dd < slots:
+        gallery.append((dd, (dd + 1) % slots))
+        dd += 1
+    crops = []
+    for k0, i0 in gallery:
+        crops.append((i0, k0))
+    s_next, f_next = ([], [])
+    kk = 0
+    while kk < slots - 1:
+        if kk % 2 == 0:
+            s_next.append(
+                lax.ppermute(s_next[-1] if s_next else vec, axis_name=mesh_ax, perm=gallery)
+            )
+        else:
+            f_next.append(lax.ppermute(f_next[-1] if f_next else vec, mesh_ax, crops))
+        kk = kk + 1
+    carry = jnp.stack([*s_next[::-1], vec, *f_next])
+    raw_out = lax.axis_index(mesh_ax) - len(s_next)
+    carry = carry[(jnp.arange(slots) - raw_out) % slots]
+    return derive_object(carry, axis_k)
 
 
 def sent_together(arrays, axis, dim, along):
@@ -186,7 +220,7 @@
     )
     rewards = over_copies(partial_reward, MP)
     gathered_elements = jnp.take(shared_trie_memo, retained_pages, axis=1)
-    gathered = lax.all_gather(gathered_elements, "group", axis=1, tiled=True)
+    gathered = sheet_write(gathered_elements, "group", 1)
     expanded = jnp.take(gathered, growth_place_mapping, axis=1)
     return (scored_rows, rewards, expanded)
 

time: 323 us -> 373 us (1.15)
  local copies, waits for them, and re-layouts: 39.9 us -> 60.8 us
  waiting for transfers between devices: 164 us -> 182 us
  starting transfers between devices: 23 us -> 35.6 us
    ppermute x0 -> x7, waiting for transfers between devices: none -> 89.1 us  [the longest x4 89.1 us: sheet_write(): lax.ppermute(s_next[-1] if s_next else vec, axis_name=mesh_ax, perm=gallery)]
    all_gather x1 -> x0, waiting for transfers between devices: 73.9 us -> none  [local(): gathered = lax.all_gather(gathered_elements, 'group', axis=1, tiled=True)]
    unnamed x33 -> x41, local copies, waits for them, and re-layouts: 1.93 us -> 13.8 us
    ppermute x0 -> x7, starting transfers between devices: none -> 9.26 us  [the longest x3 8.12 us: sheet_write(): f_next.append(lax.ppermute(f_next[-1] if f_next else vec, mesh_ax, crops))]
    all_gather x1 -> x0, local copies, waits for them, and re-layouts: 8.24 us -> none  [local(): gathered = lax.all_gather(gathered_elements, 'group', axis=1, tiled=True)]
    transpose x0 -> x1, local copies, waits for them, and re-layouts: none -> 8.21 us  [derive_object(): block_in = jnp.moveaxis(block_in, 0, dim_i)]
    gather x0 -> x1, local copies, waits for them, and re-layouts: none -> 8.06 us  [sheet_write(): carry = carry[(jnp.arange(slots) - raw_out) % slots]]
  transfers between devices with their start and end apart: 7 -> 13, of which waited for: 5 -> 8; matrix products, arithmetic and copies ran while one was open for 17% -> 21% of each run, Pallas kernels for 0% -> 0%
where the time goes in v1:
time: 373 us; the launch traced here: 372 us
  waiting for transfers between devices  182 us (49%)
  local copies, waits for them, and re-layouts  60.8 us (16%)
  matrix products  40.3 us (11%)
  starting transfers between devices  35.6 us (10%)
  other arithmetic  22.5 us (6%)
  blocking collectives  16.9 us (5%)
  between operations  14.1 us (4%)
    ppermute x4, waiting for transfers between devices, sheet_write(): lax.ppermute(s_next[-1] if s_next else vec, axis_name=mesh_ax, perm=gallery)  89.1 us
    all_to_all x1, waiting for transfers between devices, local(): lax.all_to_all(spread, MP, split_axis=3, concat_axis=1, tiled=True)  44.1 us
    reduce_scatter x1, waiting for transfers between devices, scatter_pairs(): tiles = lax.psum_scatter(tiles, core, scatter_dimension=0, tiled=True)  23.6 us
    all_gather x1, waiting for transfers between devices, sent_together(): lax.all_gather(both, axis, axis=dim, tiled=True)  19.5 us
    all_to_all x1, blocking collectives, local(): lax.all_to_all(option_latent_states, 'group', split_axis=0, concat_axis=0...  16.9 us
    all_to_all x2, starting transfers between devices, from_everyone(): return lax.all_to_all(copies, axis, split_axis=0, concat_axis=0, tiled=True)  16.5 us
    dot_general x2, matrix products, local(): jnp.einsum('rd,pd->rp', my_queries[:, head_index], path_keys, preferred_e...  15 us
    unnamed x41, local copies, waits for them, and re-layouts  13.8 us
  transfers between devices with their start and end apart: 13, of which 8 were waited for; matrix products, arithmetic and copies ran while one was open for 21% of the time, Pallas kernels for 0%

profile of v1, /device:TPU:1, one launch (start us, length us, event | category | flops | bytes accessed | tf_op | source)
XLA Modules:
  0.0 371.9 jit_solution(225709160765624638)
XLA Ops:
  7.2 16.9 %all_to_all.38 = bf16[8,32,256]{2,1,0:T(8,128)(2,1)S(1)} all-to-all(bf16[8,32,256]{2,1,0:T(8,128)(2,1)} %bitcast.165), channel_id=1, replica_groups=mesh['group'=8,'mp_0'=4,'mp_1'=4,'mp_2'=2] {'group'}, dimensions={0} | all-to-all | bytes 262144 | tf_op jit(solution)/shard_map/all_to_all | solution.py:112
  24.1 1.3 pad_maximum_fusion
  25.8 3.2 broadcast_in_dim.99
  29.0 9.6 %all-to-all-start.1 = ((bf16[2,2,128,32,128]{4,2,1,0,3:T(8,128)(2,1)}), bf16[2,2,128,32,128]{4,2,1,0,3:T(8,128)(2,1)}, u32[]{:S(2)}, u32[]{:S(2)}) async-start(bf16[2,2,128,32,128]{4,2,1,0,3:T(8,128)(2,1)} %bitcast.147), calls=%async_computation.1 | async-start | bytes 8388608 | tf_op jit(solution)/shard_map/all_to_all | solution.py:166
  38.6 6.3 %copy.104 = bf16[8192,128,2]{1,0,2:T(8,128)(2,1)} copy(bf16[8192,128,2]{0,1,2:T(8,128)(2,1)} %bitcast.157) | data formatting | bytes 8388608 | tf_op jit(solution)/shard_map/jrd,jdf->rf/dot_general | solution.py:207
  45.5 44.1 %all-to-all-done.1 = bf16[2,2,128,32,128]{4,2,1,0,3:T(8,128)(2,1)} async-done(((bf16[2,2,128,32,128]{4,2,1,0,3:T(8,128)(2,1)}), bf16[2,2,128,32,128]{4,2,1,0,3:T(8,128)(2,1)}, u32[]{:S(2)}, u32[]{:S(2)}) %all-to-all-start.1) | async-done | bytes 4194336 | tf_op jit(solution)/shard_map/all_to_all | solution.py:166
  89.6 2.5 copy.136
  92.1 2.3 fusion.67
  94.4 19.5 %all-gather.2.cloned.1.call-done = bf16[257,8192]{1,0:T(8,128)(2,1)} async-done(((bf16[257,256]{1,0:T(8,128)(2,1)}), bf16[257,8192]{1,0:T(8,128)(2,1)}) %all-gather.2.cloned.1.call-update) | async-done | bytes 4210704 | tf_op jit(solution)/shard_map/all_gather | solution.py:59
  113.9 3.1 fusion.3
  117.9 3.6 fusion.40
  121.5 1.1 broadcast_in_dim.102
  122.6 5.5 %all-to-all-start.2 = ((bf16[32,64,256]{2,1,0:T(8,128)(2,1)}), bf16[32,64,256]{2,1,0:T(8,128)(2,1)}, u32[]{:S(2)}, u32[]{:S(2)}) async-start(bf16[32,64,256]{2,1,0:T(8,128)(2,1)} %broadcast_in_dim.102), calls=%async_computation.2 | async-start | bytes 2097152 | tf_op jit(solution)/shard_map/all_to_all | solution.py:70
  128.3 5.4 %fusion.25 = bf16[256,256]{0,1:T(8,128)(2,1)S(1)} fusion(bf16[8192,256]{1,0:T(8,128)(2,1)} %param.14, f32[8192]{0:T(1024)S(1)} %bitcast.173, bf16[257,8192]{1,0:T(8,128)(2,1)} %all-gather.2.cloned.1.call-done, f32[256]{0:T(256)S(1)} %add_rsqrt_fusion), kind=kOutput, calls=%fused_computation.32 | convolution fusion | flops 1080164352 | bytes 8553472 | tf_op jit(solution)/shard_map/dot_general | solution.py:124
  135.2 7.5 %fusion.71 = (f32[256]{0:T(256)S(1)}, f32[256,8192]{1,0:T(8,128)}) fusion(bf16[8192,128]{1,0:T(8,128)(2,1)} %bitcast.160, bf16[256,2,128]{0,2,1:T(8,128)(2,1)S(1)} %bitcast.166, pred[32,8,64,128]{3,2,1,0:T(32,128)(4,1)S(1)} %bitcast.152), kind=kOutput, calls=%fused_computation.108 | convolution fusion | flops 543162112 | bytes 12649472 | tf_op jit(solution)/shard_map/rd,pd->rp/dot_general | solution.py:178
  142.7 7.5 %fusion.69 = (f32[256]{0:T(256)S(1)}, f32[256,8192]{1,0:T(8,128)}) fusion(bf16[8192,128]{1,0:T(8,128)(2,1)} %bitcast.161, bf16[256,2,128]{0,2,1:T(8,128)(2,1)S(1)} %bitcast.167, pred[32,8,64,128]{3,2,1,0:T(32,128)(4,1)S(1)} %bitcast.153), kind=kOutput, calls=%fused_computation.106 | convolution fusion | flops 543162112 | bytes 12649472 | tf_op jit(solution)/shard_map/rd,pd->rp/dot_general | solution.py:178
  151.9 1.4 fusion.70
  154.0 1.2 max.34
  156.5 7.5 %fusion.28 = f32[1,256,128]{2,1,0:T(8,128)} fusion(bf16[8192,128]{1,0:T(8,128)(2,1)} %bitcast.158, f32[256,8192]{1,0:T(8,128)} %get-tuple-element.37, f32[256]{0:T(256)} %max.34, pred[32,8,64,128]{3,2,1,0:T(32,128)(4,1)S(1)} %bitcast.154), kind=kOutput, calls=%fused_computation.33 | convolution fusion | flops 543162368 | bytes 12715008 | tf_op jit(solution)/shard_map/dot_general | solution.py:190
  164.1 7.6 %fusion.4 = (f32[256]{0:T(256)}, f32[256]{0:T(256)}) fusion(f32[256,8192]{1,0:T(8,128)S(1)} %copy-done.1, f32[256]{0:T(256)S(1)} %copy-done.5, pred[32,8,64,128]{3,2,1,0:T(32,128)(4,1)S(1)} %bitcast.155, f32[256,8192]{1,0:T(8,128)} %get-tuple-element.33, f32[256]{0:T(256)S(1)} %max.35), kind=kLoop, calls=%fused_computation.13 | loop fusion | flops 12582400 | bytes 18878464 | tf_op jit(solution)/shard_map/reduce_sum | solution.py:192
  171.7 3.7 %fusion.31 = f32[1,256,128]{2,1,0:T(8,128)} fusion(bf16[8192,128]{1,0:T(8,128)(2,1)S(1)} %bitcast.159, f32[256,8192]{1,0:T(8,128)S(1)} %bitcast.151, f32[256]{0:T(256)S(1)} %max.35, pred[32,8,64,128]{3,2,1,0:T(32,128)(4,1)S(1)} %bitcast.156), kind=kOutput, calls=%fused_computation.34 | convolution fusion | flops 543162368 | bytes 12715008 | tf_op jit(solution)/shard_map/dot_general | solution.py:190
  176.7 1.1 fusion.45
  177.8 3.5 fusion.52
  181.3 3.8 %copy.106 = f32[2,16,256,256]{3,2,1,0:T(8,128)} copy(f32[2,16,256,256]{3,2,0,1:T(8,128)S(1)} %bitcast.144) | data formatting | bytes 16777216 | tf_op jit(solution)/shard_map/transpose | solution.py:86
  185.2 23.6 %reduce-scatter.5.cloned.1.call-done = f32[16,256,256]{2,1,0:T(8,128)} async-done(((f32[32,256,256]{2,1,0:T(8,128)}), f32[16,256,256]{2,1,0:T(8,128)}) %reduce-scatter.5.cloned.1.call-update) | async-done | bytes 4194320 | tf_op jit(solution)/shard_map/reduce_scatter | solution.py:87
  209.7 1.1 collective-permute-start
  210.8 24.8 %collective-permute-done = bf16[2,2,128,1024]{3,2,0,1:T(8,128)(2,1)S(1)} collective-permute-done((bf16[2,2,128,1024]{3,2,0,1:T(8,128)(2,1)S(1)}, bf16[2,2,128,1024]{3,2,0,1:T(8,128)(2,1)S(1)}, u32[]{:S(2)}, u32[]{:S(2)}) %collective-permute-start) | collective-permute-done | bytes 1048608 | tf_op jit(solution)/shard_map/ppermute | solution.py:42
  235.6 2.7 collective-permute-start.4
  238.3 22.3 %collective-permute-done.1 = bf16[2,2,128,1024]{3,2,0,1:T(8,128)(2,1)} collective-permute-done((bf16[2,2,128,1024]{3,2,0,1:T(8,128)(2,1)S(1)}, bf16[2,2,128,1024]{3,2,0,1:T(8,128)(2,1)}, u32[]{:S(2)}, u32[]{:S(2)}) %collective-permute-start.1) | collective-permute-done | bytes 1048608 | tf_op jit(solution)/shard_map/ppermute | solution.py:42
  260.6 2.7 collective-permute-start.5
  263.3 21.5 %collective-permute-done.2 = bf16[2,2,128,1024]{3,2,0,1:T(8,128)(2,1)} collective-permute-done((bf16[2,2,128,1024]{3,2,0,1:T(8,128)(2,1)}, bf16[2,2,128,1024]{3,2,0,1:T(8,128)(2,1)}, u32[]{:S(2)}, u32[]{:S(2)}) %collective-permute-start.2) | collective-permute-done | bytes 1048608 | tf_op jit(solution)/shard_map/ppermute | solution.py:42
  285.1 2.7 collective-permute-start.6
  287.8 20.5 %collective-permute-done.3 = bf16[2,2,128,1024]{3,2,0,1:T(8,128)(2,1)} collective-permute-done((bf16[2,2,128,1024]{3,2,0,1:T(8,128)(2,1)}, bf16[2,2,128,1024]{3,2,0,1:T(8,128)(2,1)}, u32[]{:S(2)}, u32[]{:S(2)}) %collective-permute-start.3) | collective-permute-done | bytes 1048608 | tf_op jit(solution)/shard_map/ppermute | solution.py:42
  308.3 2.3 bitcast_dynamic-update-slice_fusion.6
  310.6 2.3 bitcast_dynamic-update-slice_fusion.5
  312.9 2.3 bitcast_dynamic-update-slice_fusion.4
  315.2 2.3 bitcast_dynamic-update-slice_fusion.3
  317.5 1.3 fusion.43
  318.8 2.3 bitcast_dynamic-update-slice_fusion.2
  322.2 1.1 bitcast_dynamic-update-slice_fusion
  323.3 8.1 %gather_fusion.1 = bf16[8,2,2,128,1024]{4,3,1,2,0:T(8,128)(2,1)} fusion(bf16[8,2,2,128,1024]{4,3,1,2,0:T(8,128)(2,1)} %bitcast_dynamic-update-slice_fusion, s32[1024]{0:T(1024)S(1)} %pad_clamp_fusion.1), kind=kCustom, calls=%fused_computation.1 | custom fusion | bytes 16777248 | tf_op jit(solution)/shard_map/gather | solution.py:49
  331.3 8.2 %copy.108 = bf16[2,8,2,128,1024]{4,3,2,1,0:T(8,128)(2,1)} copy(bf16[2,8,2,128,1024]{4,3,0,2,1:T(8,128)(2,1)} %bitcast.145) | data formatting | bytes 16777216 | tf_op jit(solution)/shard_map/transpose | solution.py:20
  339.5 4.0 %gather_fusion.2 = bf16[3,2,128,1024]{3,2,1,0:T(8,128)(2,1)S(1)} fusion(bf16[2,16,128,1024]{3,2,1,0:T(8,128)(2,1)} %bitcast.149, s32[1024]{0:T(1024)S(1)} %pad_clamp_fusion), kind=kCustom, calls=%fused_computation.2 | custom fusion | bytes 3145740 | tf_op jit(solution)/shard_map/jit(_take)/gather | solution.py:224
  343.8 1.3 copy.109
  345.0 1.1 multiply_reduce_fusion
  346.9 11.0 %all-to-all-start.3 = ((f32[32,1,16]{2,1,0:T(1,128)}), f32[32,1,16]{2,1,0:T(1,128)S(1)}, u32[]{:S(2)}, u32[]{:S(2)}) async-start(f32[32,1,16]{2,1,0:T(1,128)} %broadcast_in_dim.106), calls=%async_computation.4 | async-start | bytes 32768 | tf_op jit(solution)/shard_map/all_to_all | solution.py:70
  357.9 1.7 fusion.46
  359.6 5.3 %all-to-all-done.3 = f32[32,1,16]{2,1,0:T(1,128)S(1)} async-done(((f32[32,1,16]{2,1,0:T(1,128)}), f32[32,1,16]{2,1,0:T(1,128)S(1)}, u32[]{:S(2)}, u32[]{:S(2)}) %all-to-all-start.3) | async-done | bytes 2080 | tf_op jit(solution)/shard_map/all_to_all | solution.py:70
  (98 shorter events, 12.2 us)
Async XLA Ops:
  7.2 18.3 %copy-start = (bf16[2,2,128,1024]{3,2,1,0:T(8,128)(2,1)S(1)}, bf16[2,2,128,1024]{3,2,1,0:T(8,128)(2,1)}, u32[]{:S(2)}) copy-start(bf16[2,2,128,1024]{3,2,1,0:T(8,128)(2,1)} %param.18) | copy-start | bytes 3145732
  7.2 106.7 %all-gather.2.cloned.1.call-start = ((), (), s32[]{:S(2)}) async-start(), calls=%async_computation.6 | async-start | bytes 4460544 | tf_op jit(solution)/shard_map/all_gather | solution.py:59
  29.0 16.0 %copy-start.8 = (s32[16]{0:T(128)S(1)}, s32[16]{0:T(128)}, u32[]{:S(2)}) copy-start(s32[16]{0:T(128)} %param.20) | copy-start | bytes 196
  29.0 16.0 %copy-start.4 = (s32[16,32]{1,0:T(8,128)S(1)}, s32[16,32]{1,0:T(8,128)}, u32[]{:S(2)}) copy-start(s32[16,32]{1,0:T(8,128)} %param.19) | copy-start | bytes 6148
  29.0 16.3 %copy-start.9 = (s32[16]{0:T(128)S(1)}, s32[16]{0:T(128)}, u32[]{:S(2)}) copy-start(s32[16]{0:T(128)} %param.21) | copy-start | bytes 196
  29.0 60.5 %all-to-all-start.1 = ((bf16[2,2,128,32,128]{4,2,1,0,3:T(8,128)(2,1)}), bf16[2,2,128,32,128]{4,2,1,0,3:T(8,128)(2,1)}, u32[]{:S(2)}, u32[]{:S(2)}) async-start(bf16[2,2,128,32,128]{4,2,1,0,3:T(8,128)(2,1)} %bitcast.147), calls=%async_computation.1 | async-start | bytes 8388608 | tf_op jit(solution)/shard_map/all_to_all | solution.py:166
  92.0 25.9 %copy-start.11 = (bf16[8192,64]{0,1:T(8,128)(2,1)S(1)}, bf16[8192,64]{0,1:T(8,128)(2,1)}, u32[]{:S(2)}) copy-start(bf16[8192,64]{0,1:T(8,128)(2,1)} %param.15) | copy-start | bytes 3145732
  122.6 27.7 %all-to-all-start.2 = ((bf16[32,64,256]{2,1,0:T(8,128)(2,1)}), bf16[32,64,256]{2,1,0:T(8,128)(2,1)}, u32[]{:S(2)}, u32[]{:S(2)}) async-start(bf16[32,64,256]{2,1,0:T(8,128)(2,1)} %broadcast_in_dim.102), calls=%async_computation.2 | async-start | bytes 2097152 | tf_op jit(solution)/shard_map/all_to_all | solution.py:70
  128.1 80.7 %reduce-scatter.5.cloned.1.call-start = ((), (), s32[]{:S(2)}) async-start(), calls=%async_computation.7 | async-start | bytes 12582912 | tf_op jit(solution)/shard_map/reduce_scatter | solution.py:87
  142.6 7.6 %copy-start.7 = (f32[256]{0:T(256)}, f32[256]{0:T(256)S(1)}, u32[]{:S(2)}) copy-start(f32[256]{0:T(256)S(1)} %get-tuple-element.36) | copy-start | bytes 3076
  150.2 3.1 copy-start.6
  156.5 7.5 %copy-start.1 = (f32[256,8192]{1,0:T(8,128)S(1)}, f32[256,8192]{1,0:T(8,128)}, u32[]{:S(2)}) copy-start(f32[256,8192]{1,0:T(8,128)} %get-tuple-element.37) | copy-start | bytes 25165828
  156.5 7.5 %copy-start.5 = (f32[256]{0:T(256)S(1)}, f32[256]{0:T(256)}, u32[]{:S(2)}) copy-start(f32[256]{0:T(256)} %max.34) | copy-start | bytes 3076
  156.5 15.1 %slice-start = ((s8[8388608]{0:T(1024)(128)(4,1)}), s8[4194304]{0:T(1024)(128)(4,1)S(1)}, s32[]{:S(2)}) async-start(s8[8388608]{0:T(1024)(128)(4,1)} %bitcast.150), calls=%async_computation.9 | async-start | bytes 8388608
  164.1 7.6 %slice-start.1 = ((s8[8388608]{0:T(1024)(128)(4,1)}), s8[4194304]{0:T(1024)(128)(4,1)S(1)}, s32[]{:S(2)}) async-start(s8[8388608]{0:T(1024)(128)(4,1)} %bitcast.150), calls=%async_computation.10 | async-start | bytes 8388608
  164.1 7.6 %copy-start.2 = (bf16[1,32,2,128,1,128]{5,3,2,1,4,0:T(8,128)(2,1)S(1)}, bf16[1,32,2,128,1,128]{5,3,2,1,4,0:T(8,128)(2,1)}, u32[]{:S(2)}) copy-start(bf16[1,32,2,128,1,128]{5,3,2,1,4,0:T(8,128)(2,1)} %get-tuple-element.24) | copy-start | bytes 6291460
  185.1 23.8 %copy-start.12 = (s32[2]{0:T(128)S(1)}, s32[2]{0:T(128)}, u32[]{:S(2)}) copy-start(s32[2]{0:T(128)} %param.22) | copy-start | bytes 28
  185.1 99.9 %copy-start.13 = (bf16[256]{0:T(256)(128)(2,1)S(1)}, bf16[256]{0:T(256)(128)(2,1)}, u32[]{:S(2)}) copy-start(bf16[256]{0:T(256)(128)(2,1)} %param.17) | copy-start | bytes 1540
  185.1 99.9 %copy-start.14 = (s32[3]{0:T(128)S(1)}, s32[3]{0:T(128)}, u32[]{:S(2)}) copy-start(s32[3]{0:T(128)} %param.23) | copy-start | bytes 40
  185.1 99.9 %copy-start.10 = (s32[16]{0:T(128)S(1)}, s32[16]{0:T(128)}, u32[]{:S(2)}) copy-start(s32[16]{0:T(128)} %param.21) | copy-start | bytes 196
  185.1 159.9 %reduce-scatter.7.cloned.1.call-start = ((), (), s32[]{:S(2)}) async-start(), calls=%async_computation.8 | async-start | bytes 4456448
  209.7 25.9 %collective-permute-start = (bf16[2,2,128,1024]{3,2,0,1:T(8,128)(2,1)S(1)}, bf16[2,2,128,1024]{3,2,0,1:T(8,128)(2,1)S(1)}, u32[]{:S(2)}, u32[]{:S(2)}) collective-permute-start(bf16[2,2,128,1024]{3,2,0,1:T(8,128)(2,1)S(1)} %bitcast_select_fusion.1), channel_id=1, source_target_pairs={{0,32},{32,64},{64,96},{96,128},{128,160},{160,192},{192,224},{224... | collective-permute-start | bytes 3145736 | tf_op jit(solution)/shard_map/ppermute | solution.py:42
  235.6 2.7 copy-start.3
  235.6 25.0 %collective-permute-start.1 = (bf16[2,2,128,1024]{3,2,0,1:T(8,128)(2,1)S(1)}, bf16[2,2,128,1024]{3,2,0,1:T(8,128)(2,1)}, u32[]{:S(2)}, u32[]{:S(2)}) collective-permute-start(bf16[2,2,128,1024]{3,2,0,1:T(8,128)(2,1)S(1)} %collective-permute-done), channel_id=1, source_target_pairs={{0,32},{32,64},{64,96},{96,128},{128,160},{160,192},{192,224},{224... | collective-permute-start | bytes 3145736 | tf_op jit(solution)/shard_map/ppermute | solution.py:42
  235.6 25.0 %collective-permute-start.4 = (bf16[2,2,128,1024]{3,2,0,1:T(8,128)(2,1)S(1)}, bf16[2,2,128,1024]{3,2,0,1:T(8,128)(2,1)}, u32[]{:S(2)}, u32[]{:S(2)}) collective-permute-start(bf16[2,2,128,1024]{3,2,0,1:T(8,128)(2,1)S(1)} %bitcast_select_fusion.1), channel_id=1, source_target_pairs={{32,0},{64,32},{96,64},{128,96},{160,128},{192,160},{224,192},{0,2... | collective-permute-start | bytes 3145736 | tf_op jit(solution)/shard_map/ppermute | solution.py:45
  260.6 24.3 %collective-permute-start.2 = (bf16[2,2,128,1024]{3,2,0,1:T(8,128)(2,1)}, bf16[2,2,128,1024]{3,2,0,1:T(8,128)(2,1)}, u32[]{:S(2)}, u32[]{:S(2)}) collective-permute-start(bf16[2,2,128,1024]{3,2,0,1:T(8,128)(2,1)} %collective-permute-done.1), channel_id=1, source_target_pairs={{0,32},{32,64},{64,96},{96,128},{128,160},{160,192},{192,224},{224... | collective-permute-start | bytes 3145736 | tf_op jit(solution)/shard_map/ppermute | solution.py:42
  260.6 24.5 %collective-permute-start.5 = (bf16[2,2,128,1024]{3,2,0,1:T(8,128)(2,1)}, bf16[2,2,128,1024]{3,2,0,1:T(8,128)(2,1)S(1)}, u32[]{:S(2)}, u32[]{:S(2)}) collective-permute-start(bf16[2,2,128,1024]{3,2,0,1:T(8,128)(2,1)} %collective-permute-done.4), channel_id=1, source_target_pairs={{32,0},{64,32},{96,64},{128,96},{160,128},{192,160},{224,192},{0,2... | collective-permute-start | bytes 3145736 | tf_op jit(solution)/shard_map/ppermute | solution.py:45
  284.9 23.5 %collective-permute-start.3 = (bf16[2,2,128,1024]{3,2,0,1:T(8,128)(2,1)}, bf16[2,2,128,1024]{3,2,0,1:T(8,128)(2,1)}, u32[]{:S(2)}, u32[]{:S(2)}) collective-permute-start(bf16[2,2,128,1024]{3,2,0,1:T(8,128)(2,1)} %collective-permute-done.2), channel_id=1, source_target_pairs={{0,32},{32,64},{64,96},{96,128},{128,160},{160,192},{192,224},{224... | collective-permute-start | bytes 3145736 | tf_op jit(solution)/shard_map/ppermute | solution.py:42
  285.1 37.1 %collective-permute-start.6 = (bf16[2,2,128,1024]{3,2,0,1:T(8,128)(2,1)S(1)}, bf16[2,2,128,1024]{3,2,0,1:T(8,128)(2,1)S(1)}, u32[]{:S(2)}, u32[]{:S(2)}) collective-permute-start(bf16[2,2,128,1024]{3,2,0,1:T(8,128)(2,1)S(1)} %collective-permute-done.5), channel_id=1, source_target_pairs={{32,0},{64,32},{96,64},{128,96},{160,128},{192,160},{224,192},{0,2... | collective-permute-start | bytes 3145736 | tf_op jit(solution)/shard_map/ppermute | solution.py:45
  346.9 18.0 %all-to-all-start.3 = ((f32[32,1,16]{2,1,0:T(1,128)}), f32[32,1,16]{2,1,0:T(1,128)S(1)}, u32[]{:S(2)}, u32[]{:S(2)}) async-start(f32[32,1,16]{2,1,0:T(1,128)} %broadcast_in_dim.106), calls=%async_computation.4 | async-start | bytes 32768 | tf_op jit(solution)/shard_map/all_to_all | solution.py:70
Sparse Core Ops, SparseCore 0:
  25.6 88.2 all-gather.1
  185.3 23.5 reduce-scatter.4
  212.5 82.7 reduce-scatter.6
